TPU v7x, 32 devices: a whole 2x2x4 slice. The times are simulated.
32 devices in a mesh: dp: 4 (over x, y), ep: 8 (over z, core).
Axes of the slice: x: 2, y: 2, z: 4, core: 2. Of those that a mesh axis runs over, the one named last changes fastest.
Arguments:
- x: bfloat16 [4, 8, 256, 3072], P('dp', 'ep'), parts along dimension 0
- expert: int32 [4, 8, 256, 2], P('dp', 'ep'), parts along dimension 0
- slot: int32 [4, 8, 256, 2], P('dp', 'ep'), parts along dimension 0
- gate: float32 [4, 8, 256, 2], P('dp', 'ep'), parts along dimension 0
- w_gate: bfloat16 [8, 3072, 16384], P('ep')
- w_up: bfloat16 [8, 3072, 16384], P('ep')
- w_down: bfloat16 [8, 16384, 3072], P('ep')
Outputs:
- y: bfloat16 [4, 8, 256, 3072], P('dp', 'ep'), parts along dimension 0
There are 4 independent parts. A program takes and returns all parts, laid end to end along the dimension named above; an argument that names none is the same for every part.
All inputs are finite; a program needn't handle non-finite values.
Results may differ from a plain program's by a relative error of at most 0.009.
Values are sent between devices in bfloat16 or wider.
A program may use at most 2 GiB of HBM per device.

v0:
```python
import jax
import jax.numpy as jnp
from jax import lax
from jax.sharding import NamedSharding, PartitionSpec as P


def einsum(form, a, b):
    return jnp.einsum(form, a.astype(jnp.float32), b.astype(jnp.float32))


def solution(mesh):
    def placed(v, *spec):
        return lax.with_sharding_constraint(v, NamedSharding(mesh, P(*spec)))

    def step(x, expert, slot, gate, w_gate, w_up, w_down):
        experts, (tokens, top) = w_gate.shape[0], expert.shape[2:]
        slots = 5 * tokens * top // (4 * experts)
        to_expert = jax.nn.one_hot(expert, experts, dtype=jnp.bfloat16)
        to_slot = jax.nn.one_hot(slot, slots, dtype=jnp.bfloat16)
        weighted = to_expert * gate[..., None].astype(jnp.bfloat16)
        dispatch = einsum("abtke,abtkc->abtec", to_expert, to_slot).astype(jnp.bfloat16)
        combine = einsum("abtke,abtkc->abtec", weighted, to_slot).astype(jnp.bfloat16)
        z = einsum("abtec,abtd->aebcd", dispatch, x).astype(jnp.bfloat16)
        z = placed(z, "dp", None, "ep", None, None)
        z = placed(z, "dp", "ep", None, None, None)
        h = jax.nn.silu(einsum("aebcd,edf->aebcf", z, w_gate))
        h = (h * einsum("aebcd,edf->aebcf", z, w_up)).astype(jnp.bfloat16)
        out = einsum("aebcf,efd->aebcd", h, w_down).astype(jnp.bfloat16)
        out = placed(out, "dp", "ep", None, None, None)
        out = placed(out, "dp", None, "ep", None, None)
        y = einsum("abtec,aebcd->abtd", combine, out)
        return y.astype(jnp.bfloat16)

    return step
```

profile of v0, /device:TPU:0, one launch (start us, length us, event | category | flops | bytes accessed | tf_op | source)
XLA Modules:
  0.0 423.8 jit_solution(17593827540346394643)
XLA Ops:
  0.0 0.0 copy-start
  0.0 0.9 copy.3
  0.9 0.0 copy-start.3
  0.9 0.8 copy.5
  1.8 0.0 copy-done.3
  1.8 0.0 copy-start.5
  1.8 0.6 copy-done.5
  2.5 1.7 fusion.39
  4.2 0.3 copy.9
  4.5 0.0 copy-done
  4.5 1.2 fusion.22
  5.7 94.7 %all-to-all.4 = bf16[1,8,1,1,80,3072]{5,4,3,2,0,1:T(8,128)(2,1)S(1)} all-to-all(bf16[1,8,1,1,80,3072]{5,4,3,2,0,1:T(8,128)(2,1)S(1)} %fusion.22), channel_id=1, replica_groups=mesh['dp'=4,'ep'=8] {'ep'}, dimensions={1} | all-to-all | bytes 7864320 | tf_op jit(solution)/sharding_constraint;jit(solution)/sharding_constraint | solution.py:13
  100.4 0.0 copy-start.2
  100.4 1.9 copy-done.2
  102.3 73.0 %fusion.4 = f32[8,80,16384]{2,1,0:T(8,128)} fusion(bf16[1,3072,16384]{2,1,0:T(8,128)(2,1)} %param.4, bf16[1,8,1,1,80,3072]{5,4,3,2,0,1:T(8,128)(2,1)S(1)} %all-to-all.4), kind=kOutput, calls=%fused_computation.4 | convolution fusion | flops 64424509440 | bytes 146538496 | tf_op jit(solution)/aebcd,edf->aebcf/dot_general | solution.py:8
  175.3 76.7 %fusion.12.clone.8 = bf16[8,80,16384]{2,1,0:T(8,128)(2,1)} fusion(bf16[1,3072,16384]{2,1,0:T(8,128)(2,1)} %param.5, f32[8,80,16384]{2,1,0:T(8,128)} %fusion.4, bf16[1,8,1,1,80,3072]{5,4,3,2,0,1:T(8,128)(2,1)} %copy-done.2), kind=kOutput, calls=%fused_computation.13.clone.clone.clone.clone.clone.clone.clone.1 | convolution fusion | flops 64487424000 | bytes 167510016 | tf_op jit(solution)/aebcd,edf->aebcf/dot_general | solution.py:8
  251.9 0.0 copy-start.7
  252.0 0.0 copy-start.4
  252.0 0.0 copy-start.6
  252.0 0.0 copy-start.1
  252.0 74.6 %fusion.23 = bf16[1,1,8,1,80,3072]{5,4,3,1,0,2:T(8,128)(2,1)} fusion(bf16[1,16384,3072]{2,1,0:T(8,128)(2,1)} %param.6, bf16[8,80,16384]{2,1,0:T(8,128)(2,1)} %fusion.12.clone.8), kind=kOutput, calls=%fused_computation.17 | convolution fusion | flops 64426475520 | bytes 125566976 | tf_op jit(solution)/aebcf,efd->aebcd/dot_general | solution.py:8
  326.6 4.5 %all-to-all-start.1 = ((bf16[1,1,8,1,80,3072]{5,4,3,1,0,2:T(8,128)(2,1)}), bf16[1,1,8,1,80,3072]{5,4,3,1,0,2:T(8,128)(2,1)}, u32[]{:S(2)}, u32[]{:S(2)}) async-start(bf16[1,1,8,1,80,3072]{5,4,3,1,0,2:T(8,128)(2,1)} %fusion.23), calls=%async_computation.1 | async-start | bytes 7864320 | tf_op jit(solution)/sharding_constraint;jit(solution)/sharding_constraint | solution.py:13
  331.1 0.0 copy-done.7
  331.1 0.1 copy.4
  331.3 0.0 copy-done.4
  331.3 0.0 copy-done.6
  331.3 2.2 fusion.42
  333.5 0.3 copy.8
  333.8 85.3 %all-to-all-done.1 = bf16[1,1,8,1,80,3072]{5,4,3,1,0,2:T(8,128)(2,1)} async-done(((bf16[1,1,8,1,80,3072]{5,4,3,1,0,2:T(8,128)(2,1)}), bf16[1,1,8,1,80,3072]{5,4,3,1,0,2:T(8,128)(2,1)}, u32[]{:S(2)}, u32[]{:S(2)}) %all-to-all-start.1) | async-done | bytes 3932192 | tf_op jit(solution)/sharding_constraint;jit(solution)/sharding_constraint | solution.py:13
  419.1 4.7 %fusion.35 = bf16[1,1,256,3072]{3,2,1,0:T(8,128)(2,1)} fusion(bf16[1,1,8,1,80,3072]{5,4,3,1,0,2:T(8,128)(2,1)} %all-to-all-done.1, bf16[256,8,80]{0,2,1:T(8,128)(2,1)S(1)} %copy.8), kind=kOutput, calls=%fused_computation.23 | convolution fusion | flops 1007419392 | bytes 5832704 | tf_op jit(solution)/abtec,aebcd->abtd/dot_general | solution.py:8
  423.8 0.0 copy-done.1
  (1 shorter events, 0.0 us)
Async XLA Ops:
  0.0 4.5 %copy-start = (bf16[1,1,256,3072]{3,2,1,0:T(8,128)(2,1)S(1)}, bf16[1,1,256,3072]{3,2,1,0:T(8,128)(2,1)}, u32[]{:S(2)}) copy-start(bf16[1,1,256,3072]{3,2,1,0:T(8,128)(2,1)} %param.3) | copy-start | bytes 4718596
  0.9 0.9 copy-start.3
  1.8 0.7 copy-start.5
  100.4 1.9 copy-start.2
  251.9 79.1 %copy-start.7 = (f32[1,1,256,2]{2,3,1,0:T(2,128)S(1)}, f32[1,1,256,2]{2,3,1,0:T(2,128)}, u32[]{:S(2)}) copy-start(f32[1,1,256,2]{2,3,1,0:T(2,128)} %param.1) | copy-start | bytes 6148
  252.0 79.3 %copy-start.4 = (s32[256,2]{1,0:T(8,128)S(1)}, s32[256,2]{1,0:T(8,128)}, u32[]{:S(2)}) copy-start(s32[256,2]{1,0:T(8,128)} %copy-done.3) | copy-start | bytes 6148
  252.0 79.3 %copy-start.6 = (s32[256,2]{1,0:T(8,128)S(1)}, s32[256,2]{1,0:T(8,128)}, u32[]{:S(2)}) copy-start(s32[256,2]{1,0:T(8,128)} %copy-done.5) | copy-start | bytes 6148
  252.0 171.9 %copy-start.1 = (bf16[1,1,256,3072]{3,2,1,0:T(8,128)(2,1)S(1)}, bf16[1,1,256,3072]{3,2,1,0:T(8,128)(2,1)}, u32[]{:S(2)}) copy-start(bf16[1,1,256,3072]{3,2,1,0:T(8,128)(2,1)} %param.3) | copy-start | bytes 4718596
  326.6 92.6 %all-to-all-start.1 = ((bf16[1,1,8,1,80,3072]{5,4,3,1,0,2:T(8,128)(2,1)}), bf16[1,1,8,1,80,3072]{5,4,3,1,0,2:T(8,128)(2,1)}, u32[]{:S(2)}, u32[]{:S(2)}) async-start(bf16[1,1,8,1,80,3072]{5,4,3,1,0,2:T(8,128)(2,1)} %fusion.23), calls=%async_computation.1 | async-start | bytes 7864320 | tf_op jit(solution)/sharding_constraint;jit(solution)/sharding_constraint | solution.py:13
where the time goes:
time: 424 us
  matrix products  234 us (55%)
  blocking collectives  94.7 us (22%)
  waiting for transfers between devices  85.3 us (20%)
  local copies, waits for them, and re-layouts  5.09 us (1%)
  starting transfers between devices  4.52 us (1%)
    dot_general x7, matrix products, einsum(): return jnp.einsum(form, a.astype(jnp.float32), b.astype(jnp.float32))  234 us
    another operation x1, blocking collectives, placed(): return lax.with_sharding_constraint(v, NamedSharding(mesh, P(*spec)))  94.7 us
    another operation x1, waiting for transfers between devices, placed(): return lax.with_sharding_constraint(v, NamedSharding(mesh, P(*spec)))  85.3 us
  transfers between devices with their start and end apart: 1, of which 1 were waited for; matrix products, arithmetic and copies ran while one was open for 1% of the time, Pallas kernels for 0%

commit v1 on v0

v1 whole, which is shorter than its diff:
```python
import functools

import jax
import jax.numpy as jnp
from jax import lax
from jax.experimental import pallas as pl
from jax.experimental.pallas import tpu as pltpu
from jax.sharding import PartitionSpec as P

MESH = pl.DeviceIdType.MESH
TF = 256
TD = 256
GB = 4
DB = 4
KB = 4


def flipped(me, r):
    bits = [me % 2, (me // 2) % 2, me // 4]
    return sum(((1 - b) if (r >> i) & 1 else b) * (1 << i) for i, b in enumerate(bits))


def kernel(
    z_ref, wg_ref, wu_ref, wd_ref, wc_ref, y_ref,
    zbuf, h, osend, orecv, wgb, wub, wdb, g0, g1, u0, u1, acc, ybuf,
    wg_sem, wu_sem, wd_sem, zs_sem, zr_sem, os_sem, or_sem, own_sem, y_sem,
):
    members, slots, d = z_ref.shape
    ff = wg_ref.shape[1]
    rows = members * slots
    half = rows // 2
    tiles, chunks, kd = ff // TF, d // TD, ff // KB
    me = lax.axis_index("ep")
    peer = [flipped(me, r) for r in range(members)]

    def fetch_g(i):
        tile, b = i % tiles, i % GB
        cols = pl.ds(pl.multiple_of(tile * TF, TF), TF)
        return (
            pltpu.make_async_copy(wg_ref.at[:, cols], wgb.at[b], wg_sem.at[b]),
            pltpu.make_async_copy(wu_ref.at[:, cols], wub.at[b], wu_sem.at[b]),
        )

    def fetch_d(i):
        c, k, b = i // KB, i % KB, i % DB
        cols = pl.ds(pl.multiple_of(c * TD, TD), TD)
        deep = pl.ds(pl.multiple_of(k * kd, kd), kd)
        return pltpu.make_async_copy(wd_ref.at[deep, cols], wdb.at[b], wd_sem.at[b])

    def begin(copies):
        for c in copies:
            c.start()

    for i in range(GB - 1):
        begin(fetch_g(i))

    barrier = pltpu.get_barrier_semaphore()
    for r in range(1, members):
        pl.semaphore_signal(barrier, inc=1, device_id={"ep": peer[r]}, device_id_type=MESH)
    own = pltpu.make_async_copy(z_ref.at[0], zbuf.at[pl.ds(0, slots)], own_sem)
    own.start()
    pl.semaphore_wait(barrier, members - 1)

    def send_z(r):
        return pltpu.make_async_remote_copy(
            src_ref=z_ref.at[r],
            dst_ref=zbuf.at[pl.ds(r * slots, slots)],
            send_sem=zs_sem.at[r],
            recv_sem=zr_sem.at[r],
            device_id={"ep": peer[r]},
            device_id_type=MESH,
        )

    order = [2, 3, 1, 6, 7, 4, 5]
    for r in order:
        send_z(r).start()

    def gate_up(first, base):
        gs, us = (g0, g1), (u0, u1)

        def activate(step, p):
            cols = pl.ds(pl.multiple_of(step * TF, TF), TF)
            h[pl.ds(base, half), cols] = (jax.nn.silu(gs[p][...]) * us[p][...]).astype(h.dtype)

        def one(i, p, last):
            @pl.when(i + GB - 1 < last)
            def _():
                begin(fetch_g(i + GB - 1))

            for c in fetch_g(i):
                c.wait()
            b = i % GB
            z = zbuf[pl.ds(base, half), :]
            activate(lax.max(i - first - 1, 0), 1 - p)
            gs[p][...] = jnp.dot(z, wgb[b], preferred_element_type=jnp.float32)
            us[p][...] = jnp.dot(z, wub[b], preferred_element_type=jnp.float32)

        def pair(j, _):
            one(first + 2 * j, 0, 2 * tiles)
            one(first + 2 * j + 1, 1, 2 * tiles)
            return 0

        lax.fori_loop(0, tiles // 2, pair, 0)
        activate(tiles - 1, 1)

    g1[...] = jnp.zeros_like(g1)
    u1[...] = jnp.zeros_like(u1)

    own.wait()
    for r in range(1, members // 2):
        send_z(r).wait_recv()
    gate_up(0, 0)
    for i in range(DB - 1):
        fetch_d(i).start()
    for r in range(members // 2, members):
        send_z(r).wait_recv()
    gate_up(tiles, half)

    def send_o(c, r):
        return pltpu.make_async_remote_copy(
            src_ref=osend.at[c, pl.ds(r * slots, slots)],
            dst_ref=orecv.at[c, pl.ds(r * slots, slots)],
            send_sem=os_sem.at[c, r],
            recv_sem=or_sem.at[c, r],
            device_id={"ep": peer[r]},
            device_id_type=MESH,
        )

    def send_chunk(c):
        for r in (6, 7, 4, 5, 2, 3, 1):
            send_o(c, r).start()

    def down(c, _):
        for k in range(KB):
            i = c * KB + k

            @pl.when(i + DB - 1 < chunks * KB)
            def _():
                fetch_d(i + DB - 1).start()

            fetch_d(i).wait()
            part = jnp.dot(h[:, k * kd:(k + 1) * kd], wdb[i % DB], preferred_element_type=jnp.float32)
            if k == 0:
                acc[...] = part

                @pl.when(c > 0)
                def _():
                    send_chunk(c - 1)
            elif k < KB - 1:
                acc[...] += part
            else:
                out = (acc[...] + part).astype(osend.dtype)
                osend[c] = out
                orecv[c, pl.ds(0, slots), :] = out[:slots]
        return 0

    lax.fori_loop(0, chunks, down, 0)
    send_chunk(chunks - 1)

    def put_y(c):
        cols = pl.ds(pl.multiple_of(c * TD, TD), TD)
        return pltpu.make_async_copy(ybuf.at[c], y_ref.at[:, cols], y_sem.at[c])

    def combine(c, _):
        for r in range(1, members):
            send_o(c, r).wait_recv()
        ybuf[c] = jnp.dot(wc_ref[...], orecv[c], preferred_element_type=jnp.float32).astype(ybuf.dtype)
        put_y(c).start()
        return 0

    lax.fori_loop(0, chunks, combine, 0)

    def drain(c, _):
        for r in range(1, members):
            send_o(c, r).wait_send()
        put_y(c).wait()
        return 0

    for r in range(1, members):
        send_z(r).wait_send()
    lax.fori_loop(0, chunks, drain, 0)


def experts(z, wg, wu, wd, wc):
    members, slots, d = z.shape
    ff, tokens = wg.shape[1], wc.shape[0]
    rows, chunks = members * slots, d // TD
    bf16, f32 = jnp.bfloat16, jnp.float32
    dma = pltpu.SemaphoreType.DMA
    hbm = pl.BlockSpec(memory_space=pl.ANY)
    half = rows // 2
    return pl.pallas_call(
        kernel,
        out_shape=jax.ShapeDtypeStruct((tokens, d), bf16),
        in_specs=[hbm, hbm, hbm, hbm, pl.BlockSpec(memory_space=pltpu.VMEM)],
        out_specs=hbm,
        scratch_shapes=[
            pltpu.VMEM((rows, d), bf16),
            pltpu.VMEM((rows, ff), bf16),
            pltpu.VMEM((chunks, rows, TD), bf16),
            pltpu.VMEM((chunks, rows, TD), bf16),
            pltpu.VMEM((GB, d, TF), bf16),
            pltpu.VMEM((GB, d, TF), bf16),
            pltpu.VMEM((DB, ff // KB, TD), bf16),
            pltpu.VMEM((half, TF), f32),
            pltpu.VMEM((half, TF), f32),
            pltpu.VMEM((half, TF), f32),
            pltpu.VMEM((half, TF), f32),
            pltpu.VMEM((rows, TD), f32),
            pltpu.VMEM((chunks, tokens, TD), bf16),
            dma((GB,)), dma((GB,)), dma((DB,)),
            dma((members,)), dma((members,)),
            dma((chunks, members)), dma((chunks, members)),
            dma, dma((chunks,)),
        ],
        compiler_params=pltpu.CompilerParams(
            collective_id=0, has_side_effects=True, vmem_limit_bytes=66_000_000
        ),
        cost_estimate=pl.CostEstimate(
            flops=6 * rows * d * ff, bytes_accessed=6 * d * ff, transcendentals=rows * ff
        ),
    )(z, wg, wu, wd, wc)


def solution(mesh):
    def step(x, expert, slot, gate, wg, wu, wd):
        x, expert, slot, gate = x[0, 0], expert[0, 0], slot[0, 0], gate[0, 0]
        tokens, top = expert.shape
        members = mesh.shape["ep"]
        slots = 5 * tokens * top // (4 * members)
        me = lax.axis_index("ep")
        relative = jnp.bitwise_xor(expert, me)
        to_expert = jax.nn.one_hot(relative, members, dtype=jnp.bfloat16)
        to_slot = jax.nn.one_hot(slot, slots, dtype=jnp.bfloat16)
        weighted = to_expert * gate[..., None].astype(jnp.bfloat16)
        f32 = jnp.float32
        dispatch = jnp.einsum("tke,tkc->ect", to_expert.astype(f32), to_slot.astype(f32)).astype(jnp.bfloat16)
        combine = jnp.einsum("tke,tkc->tec", weighted.astype(f32), to_slot.astype(f32)).astype(jnp.bfloat16)
        z = jnp.einsum("ect,td->ecd", dispatch.astype(f32), x.astype(f32)).astype(jnp.bfloat16)
        y = experts(z, wg[0], wu[0], wd[0], combine.reshape(tokens, members * slots))
        return y[None, None]

    tok, exp = P("dp", "ep"), P("ep")
    return jax.shard_map(
        step, mesh=mesh, in_specs=(tok, tok, tok, tok, exp, exp, exp), out_specs=tok, check_vma=False
    )
```

time: 424 us -> 361 us (0.85)
  Pallas kernels: 0 us -> 345 us
  matrix products: 234 us -> 6.91 us
  blocking collectives: 94.7 us -> 0 us
  waiting for transfers between devices: 85.3 us -> 0 us
  starting transfers between devices: 4.52 us -> 0 us
    pallas_call x0 -> x1, Pallas kernels: none -> 345 us  [experts(): pl.pallas_call(kernel, out_shape=jax.ShapeDtypeStruct((tokens, d), bf16),...]
    dot_general x7 -> x3, matrix products: 234 us -> 6.91 us  [the longest x1 3.07 us: step(): jnp.einsum('ect,td->ecd', dispatch.astype(f32), x.astype(f32))]
    another operation x1 -> x0, blocking collectives: 94.7 us -> none  [placed(): return lax.with_sharding_constraint(v, NamedSharding(mesh, P(*spec)))]
    another operation x1 -> x0, waiting for transfers between devices: 85.3 us -> none  [placed(): return lax.with_sharding_constraint(v, NamedSharding(mesh, P(*spec)))]
    another operation x1 -> x0, starting transfers between devices: 4.52 us -> none  [placed(): return lax.with_sharding_constraint(v, NamedSharding(mesh, P(*spec)))]
  transfers between devices with their start and end apart: 1 -> 0, of which waited for: 1 -> 0; matrix products, arithmetic and copies ran while one was open for 1% -> 0% of each run, Pallas kernels for 0% -> 0%
where the time goes in v1:
time: 361 us; the launch traced here: 359 us
  Pallas kernels  345 us (96%)
  matrix products  6.91 us (2%)
  local copies, waits for them, and re-layouts  5.3 us (1%)
    pallas_call x1, Pallas kernels, experts(): pl.pallas_call(kernel, out_shape=jax.ShapeDtypeStruct((tokens, d), bf16),...  345 us

profile of v1, /device:TPU:0, one launch (start us, length us, event | category | flops | bytes accessed | tf_op | source)
XLA Modules:
  0.0 358.8 jit_solution(5005303731756669006)
XLA Ops:
  0.0 0.7 convert_bitcast_fusion
  0.7 0.7 xor_bitcast_fusion
  1.4 0.1 copy.13
  1.5 0.1 copy.12
  1.7 0.8 copy.11
  2.5 2.2 convolution_convert_fusion.1
  4.7 0.0 copy-start
  4.7 0.3 copy.14
  5.0 0.9 copy.15.wc_ref
  5.9 1.6 fusion.4
  7.6 0.3 copy.16
  7.9 0.0 copy-done
  7.9 3.1 convolution_convert_fusion.z_ref
  11.0 345.2 %shard_map.73 = bf16[256,3072]{1,0:T(8,128)(2,1)} custom-call(bf16[8,80,3072]{2,1,0:T(8,128)(2,1)} %convolution_convert_fusion.z_ref, bf16[3072,16384]{1,0:T(8,128)(2,1)} %bitcast.5.wg_ref, bf16[3072,16384]{1,0:T(8,128)(2,1)} %bitcast.6.wu_ref, bf16[16384,3072]{1,0:T(8,128)(2,1)} %bitcast.7.wd_ref, bf16[256,640]{1,0:T(8,128)(2,1)} %copy.15.wc_ref), custom_call_target="tpu_custom_call" | custom-call | flops 193273528320 | bytes 301989888 | tf_op jit(solution)/shard_map/pallas_call | solution.py:192
  356.2 2.7 copy.18
Async XLA Ops:
  4.7 3.2 copy-start

commit v2 on v1

v2 whole, which is shorter than its diff:
```python
import functools

import jax
import jax.numpy as jnp
from jax import lax
from jax.experimental import pallas as pl
from jax.experimental.pallas import tpu as pltpu
from jax.sharding import PartitionSpec as P

MESH = pl.DeviceIdType.MESH
TF = 512
TD = 256
GB = 3
DB = 3
KB = 4


def flipped(me, r):
    bits = [me % 2, (me // 2) % 2, me // 4]
    return sum(((1 - b) if (r >> i) & 1 else b) * (1 << i) for i, b in enumerate(bits))


def kernel(
    members,
    x_ref, expert_ref, slot_ref, gate_ref, wg_ref, wu_ref, wd_ref, y_ref,
    zbuf, h, osend, orecv, wgb, wub, wdb, acc0, acc1, ybuf, wc,
    wg_sem, wu_sem, wd_sem, zs_sem, zr_sem, os_sem, or_sem, x_sem, y_sem,
):
    tokens, d = x_ref.shape
    ff = wg_ref.shape[1]
    rows = zbuf.shape[0]
    slots = rows // members
    half = rows // 2
    tiles, chunks, kd = ff // TF, d // TD, ff // KB
    me = lax.axis_index("ep")
    peer = [flipped(me, r) for r in range(members)]

    def fetch_g(i):
        tile, b = i % tiles, i % GB
        cols = pl.ds(pl.multiple_of(tile * TF, TF), TF)
        return (
            pltpu.make_async_copy(wg_ref.at[:, cols], wgb.at[b], wg_sem.at[b]),
            pltpu.make_async_copy(wu_ref.at[:, cols], wub.at[b], wu_sem.at[b]),
        )

    def fetch_d(i):
        c, k, b = i // KB, i % KB, i % DB
        cols = pl.ds(pl.multiple_of(c * TD, TD), TD)
        deep = pl.ds(pl.multiple_of(k * kd, kd), kd)
        return pltpu.make_async_copy(wd_ref.at[deep, cols], wdb.at[b], wd_sem.at[b])

    def begin(copies):
        for c in copies:
            c.start()

    load_x = pltpu.make_async_copy(x_ref, ybuf, x_sem)
    load_x.start()
    for i in range(GB - 1):
        begin(fetch_g(i))

    barrier = pltpu.get_barrier_semaphore()
    for r in range(1, members):
        pl.semaphore_signal(barrier, inc=1, device_id={"ep": peer[r]}, device_id_type=MESH)
    place = [
        jnp.where(slot_ref[j:j + 1, :] < slots, expert_ref[j:j + 1, :] * slots + slot_ref[j:j + 1, :], -1)
        for j in range(expert_ref.shape[0])
    ]
    line = lax.broadcasted_iota(jnp.int32, (slots, tokens), 0)

    def chosen(r, values):
        here = line + peer[r] * slots
        return sum(jnp.where(here == p, v, 0.0) for p, v in zip(place, values))

    def rows_of(r):
        pick = chosen(r, [1.0] * len(place)).astype(x_ref.dtype)
        return jnp.dot(pick, ybuf[...], preferred_element_type=jnp.float32).astype(zbuf.dtype)

    def send_z(r):
        return pltpu.make_async_remote_copy(
            src_ref=osend.at[pl.ds(r * slots, slots)],
            dst_ref=zbuf.at[pl.ds(r * slots, slots)],
            send_sem=zs_sem.at[r],
            recv_sem=zr_sem.at[r],
            device_id={"ep": peer[r]},
            device_id_type=MESH,
        )

    load_x.wait()
    pl.semaphore_wait(barrier, members - 1)
    groups = [(2, 3), (6, 7), (4, 5), (1, 0)]
    for now, before in zip(groups + [()], [()] + groups):
        for r in now:
            if r == 0:
                zbuf[0:slots, :] = rows_of(r)
            else:
                osend[r * slots:(r + 1) * slots, :] = rows_of(r)
        for r in before:
            if r > 0:
                send_z(r).start()

    weights = [gate_ref[j:j + 1, :].astype(wc.dtype).astype(jnp.float32) for j in range(len(place))]
    table = jnp.concatenate([chosen(r, weights) for r in range(members)], axis=0)
    wc[...] = table.T.astype(wc.dtype)

    def gate_up(first, base):
        def one(j, _):
            i = first + j

            @pl.when(i + GB - 1 < 2 * tiles)
            def _():
                begin(fetch_g(i + GB - 1))

            for c in fetch_g(i):
                c.wait()
            b = i % GB
            z = zbuf[pl.ds(base, half), :]
            g = jnp.dot(z, wgb[b], preferred_element_type=jnp.float32)
            u = jnp.dot(z, wub[b], preferred_element_type=jnp.float32)
            cols = pl.ds(pl.multiple_of(j * TF, TF), TF)
            h[pl.ds(base, half), cols] = (jax.nn.silu(g) * u).astype(h.dtype)
            return 0

        lax.fori_loop(0, tiles, one, 0)

    for r in range(1, members // 2):
        send_z(r).wait_recv()
    gate_up(0, 0)
    for i in range(DB - 1):
        fetch_d(i).start()
    for r in range(members // 2, members):
        send_z(r).wait_recv()
    gate_up(tiles, half)
    for r in range(1, members):
        send_z(r).wait_send()

    def chunk(c):
        return pl.ds(pl.multiple_of(c * TD, TD), TD)

    def send_o(c, r):
        return pltpu.make_async_remote_copy(
            src_ref=osend.at[pl.ds(r * slots, slots), chunk(c)],
            dst_ref=orecv.at[pl.ds(r * slots, slots), chunk(c)],
            send_sem=os_sem.at[c, r],
            recv_sem=or_sem.at[c, r],
            device_id={"ep": peer[r]},
            device_id_type=MESH,
        )

    def send_chunk(c):
        for r in (6, 7, 4, 5, 2, 3, 1):
            send_o(c, r).start()

    def down(c, _):
        for k in range(KB):
            i = c * KB + k

            @pl.when(i + DB - 1 < chunks * KB)
            def _():
                fetch_d(i + DB - 1).start()

            fetch_d(i).wait()
            w = wdb[i % DB]
            for s, acc in enumerate((acc0, acc1)):
                deep = h[s * half:(s + 1) * half, k * kd:(k + 1) * kd]
                part = jnp.dot(deep, w, preferred_element_type=jnp.float32)
                if k == 0:
                    acc[...] = part
                elif k < KB - 1:
                    acc[...] += part
                else:
                    out = (acc[...] + part).astype(osend.dtype)
                    osend[pl.ds(s * half, half), chunk(c)] = out
                    if s == 0:
                        orecv[pl.ds(0, slots), chunk(c)] = out[:slots]
            if k == 0:

                @pl.when(c > 0)
                def _():
                    send_chunk(c - 1)

        return 0

    lax.fori_loop(0, chunks, down, 0)
    send_chunk(chunks - 1)

    def put_y(c):
        return pltpu.make_async_copy(ybuf.at[:, chunk(c)], y_ref.at[:, chunk(c)], y_sem.at[c])

    def combine(c, _):
        for r in range(1, members):
            send_o(c, r).wait_recv()
        ybuf[:, chunk(c)] = jnp.dot(
            wc[...], orecv[:, chunk(c)], preferred_element_type=jnp.float32
        ).astype(ybuf.dtype)
        put_y(c).start()
        return 0

    lax.fori_loop(0, chunks, combine, 0)

    def drain(c, _):
        for r in range(1, members):
            send_o(c, r).wait_send()
        put_y(c).wait()
        return 0

    lax.fori_loop(0, chunks, drain, 0)


def experts(members, slots, x, expert, slot, gate, wg, wu, wd):
    tokens, d = x.shape
    ff = wg.shape[1]
    rows, chunks = members * slots, d // TD
    bf16, f32 = jnp.bfloat16, jnp.float32
    dma = pltpu.SemaphoreType.DMA
    hbm = pl.BlockSpec(memory_space=pl.ANY)
    vmem = pl.BlockSpec(memory_space=pltpu.VMEM)
    half = rows // 2
    return pl.pallas_call(
        functools.partial(kernel, members),
        out_shape=jax.ShapeDtypeStruct((tokens, d), bf16),
        in_specs=[hbm, vmem, vmem, vmem, hbm, hbm, hbm],
        out_specs=hbm,
        scratch_shapes=[
            pltpu.VMEM((rows, d), bf16),
            pltpu.VMEM((rows, ff), bf16),
            pltpu.VMEM((rows, d), bf16),
            pltpu.VMEM((rows, d), bf16),
            pltpu.VMEM((GB, d, TF), bf16),
            pltpu.VMEM((GB, d, TF), bf16),
            pltpu.VMEM((DB, ff // KB, TD), bf16),
            pltpu.VMEM((half, TD), f32),
            pltpu.VMEM((half, TD), f32),
            pltpu.VMEM((tokens, d), bf16),
            pltpu.VMEM((tokens, rows), bf16),
            dma((GB,)), dma((GB,)), dma((DB,)),
            dma((members,)), dma((members,)),
            dma((chunks, members)), dma((chunks, members)),
            dma, dma((chunks,)),
        ],
        compiler_params=pltpu.CompilerParams(
            collective_id=0, has_side_effects=True, vmem_limit_bytes=67_000_000
        ),
        cost_estimate=pl.CostEstimate(
            flops=6 * rows * d * ff, bytes_accessed=6 * d * ff, transcendentals=rows * ff
        ),
    )(x, expert, slot, gate, wg, wu, wd)


def solution(mesh):
    def step(x, expert, slot, gate, wg, wu, wd):
        tokens, top = expert.shape[2:]
        members = mesh.shape["ep"]
        slots = 5 * tokens * top // (4 * members)
        y = experts(
            members, slots, x[0, 0], expert[0, 0].T, slot[0, 0].T, gate[0, 0].T, wg[0], wu[0], wd[0]
        )
        return y[None, None]

    tok, exp = P("dp", "ep"), P("ep")
    return jax.shard_map(
        step, mesh=mesh, in_specs=(tok, tok, tok, tok, exp, exp, exp), out_specs=tok, check_vma=False
    )
```

time: 361 us -> 269 us (0.75)
  Pallas kernels: 345 us -> 266 us
  matrix products: 6.91 us -> 0 us
    pallas_call x1, Pallas kernels: 345 us -> 266 us  [experts(): pl.pallas_call(functools.partial(kernel, members), out_shape=jax.ShapeDty...]
    dot_general x3 -> x0, matrix products: 6.91 us -> none  [the longest x1 3.07 us: step(): jnp.einsum('ect,td->ecd', dispatch.astype(f32), x.astype(f32))]
where the time goes in v2:
time: 269 us
  Pallas kernels  266 us (99%)
    pallas_call x1, Pallas kernels, experts(): pl.pallas_call(functools.partial(kernel, members), out_shape=jax.ShapeDty...  266 us

profile of v2, /device:TPU:0, one launch (start us, length us, event | category | flops | bytes accessed | tf_op | source)
XLA Modules:
  0.0 268.9 jit_solution(11460093039775794605)
XLA Ops:
  0.0 266.3 %shard_map.73 = bf16[256,3072]{1,0:T(8,128)(2,1)} custom-call(bf16[256,3072]{1,0:T(8,128)(2,1)} %bitcast.15, s32[2,256]{1,0:T(2,128)} %bitcast.16, s32[2,256]{1,0:T(2,128)} %bitcast.17, f32[2,256]{1,0:T(2,128)} %bitcast.18, bf16[3072,16384]{1,0:T(8,128)(2,1)} %bitcast.7.wg_ref, bf16[3072,16384]{1,0:T(8,128)(2,1)} %bitcast.8.wu_ref, ...), custom_call_target="tpu_custom_call" | custom-call | flops 193273528320 | bytes 301989888 | tf_op jit(solution)/shard_map/pallas_call | solution.py:218
  266.3 2.7 copy.9
